TPU v7x, 8 devices: a whole 2x2x1 slice. The times are simulated.
8 devices in a mesh: batch: 1 (over z), row: 2 (over y), col: 4 (over x, core).
Axes of the slice: x: 2, y: 2, z: 1, core: 2. Of those that a mesh axis runs over, the one named last changes fastest.
Arguments:
- a_mat: bfloat16 [5120, 32768], P(('batch', 'row'), 'col')
Outputs:
- output: bfloat16 [5120, 5120], P(('batch', 'row'), 'col')
All inputs are finite; a program needn't handle non-finite values.
Results may differ from a plain program's by a relative error of at most 0.001.
Values are sent between devices in bfloat16 or wider.
A program may use at most 1 GiB of HBM per device.

v0:
```python
import jax
import jax.numpy as jnp
from jax import lax
from jax.sharding import PartitionSpec as P

BLOCK = 256


def lower_part(row_panel, col_panel, row_step, row_pos, col_step, col_pos):
    row_blocks = row_panel.shape[0] // BLOCK
    col_blocks = col_panel.shape[0] // BLOCK
    col_total = col_panel.shape[0]
    band_size = max(1, row_blocks // 8)
    col_local = jnp.arange(col_total)
    col_index = ((col_local // BLOCK) * col_step + col_pos) * BLOCK + col_local % BLOCK
    pieces = []
    for first_blk in range(0, row_blocks, band_size):
        last_blk = min(first_blk + band_size, row_blocks)
        col_width = BLOCK * min(col_blocks, (last_blk * row_step - 1) // col_step + 1)
        product = lax.dot_general(row_panel[first_blk * BLOCK:last_blk * BLOCK], col_panel[:col_width], (((1,), (1,)), ((), ())), preferred_element_type=jnp.float32)
        row_local = jnp.arange(first_blk * BLOCK, last_blk * BLOCK)
        row_index = ((row_local // BLOCK) * row_step + row_pos) * BLOCK + row_local % BLOCK
        kept_vals = jnp.where(row_index[:, None] >= col_index[None, :col_width], product, 0.0).astype(jnp.bfloat16)
        pieces.append(jnp.pad(kept_vals, ((0, 0), (0, col_total - col_width))))
    return jnp.concatenate(pieces, axis=0)


def solution(mesh):
    row_count = mesh.shape['row']
    col_count = mesh.shape['col']

    def local_fn(a_local):
        local_rows, m_local = a_local.shape
        n_total = local_rows * row_count
        row_pos = lax.axis_index('row')
        col_pos = lax.axis_index('col')
        row_panel = lax.all_gather(a_local, 'col', axis=1, tiled=True)
        gathered = lax.all_gather(a_local.reshape(local_rows // BLOCK, BLOCK, m_local), 'row', axis=1)
        grouped = gathered.reshape(n_total // (BLOCK * col_count), col_count, BLOCK, m_local)
        swapped = lax.all_to_all(grouped, 'col', 1, 3, tiled=True)
        col_panel = swapped.reshape(n_total // col_count, m_local * col_count)
        return lower_part(row_panel, col_panel, row_count, row_pos, col_count, col_pos)

    part_spec = P(('batch', 'row'), 'col')
    return jax.shard_map(local_fn, mesh=mesh, in_specs=(part_spec,), out_specs=part_spec, check_vma=False)
```

profile of v0, /device:TPU:1, one launch (start us, length us, event | category | flops | bytes accessed | tf_op | source)
XLA Modules:
  0.0 3864.7 jit_solution(11121026029110378323)
XLA Ops:
  6.5 0.0 all-gather.5.cloned.1.call-start
  6.5 0.7 all-gather.5.cloned.1.call-update
  7.3 0.0 all-gather.3.cloned.1.call-start
  7.3 0.7 all-gather.3.cloned.1.call-update
  8.0 954.4 %all-gather.5.cloned.1.call-done = bf16[10,2,256,8192]{3,2,1,0:T(8,128)(2,1)} async-done(((bf16[10,1,256,8192]{3,2,1,0:T(8,128)(2,1)}), bf16[10,2,256,8192]{3,2,1,0:T(8,128)(2,1)}) %all-gather.5.cloned.1.call-update) | async-done | bytes 83886096 | tf_op jit(solution)/shard_map/all_gather | solution.py:38
  962.4 55.4 %copy.7 = bf16[5,4,256,8192]{3,2,0,1:T(8,128)(2,1)} copy(bf16[5,4,256,8192]{3,2,1,0:T(8,128)(2,1)} %bitcast.1) | data formatting | bytes 167772160 | tf_op jit(solution)/shard_map/reshape | solution.py:39
  1017.8 18.2 all-to-all-start
  1035.9 0.6 slice.96
  1036.5 0.6 slice.100
  1037.1 0.6 slice.104
  1037.7 0.0 copy-done
  1037.7 0.6 slice.108
  1038.3 0.5 fusion.99
  1038.8 0.6 fusion.101
  1039.4 0.6 fusion.103
  1040.0 0.6 fusion.105
  1040.6 0.6 fusion.107
  1041.2 1773.9 %all-to-all-done = bf16[5,4,256,8192]{3,2,0,1:T(8,128)(2,1)} async-done(((bf16[5,4,256,8192]{3,2,0,1:T(8,128)(2,1)}), bf16[5,4,256,8192]{3,2,0,1:T(8,128)(2,1)}, u32[]{:S(2)}, u32[]{:S(2)}) %all-to-all-start) | async-done | bytes 83886112 | tf_op jit(solution)/shard_map/all_to_all | solution.py:40
  2815.1 99.1 %copy.8 = bf16[5,4,256,8192]{2,3,1,0:T(8,128)(2,1)} copy(bf16[5,4,256,8192]{3,2,0,1:T(8,128)(2,1)} %all-to-all-done) | data formatting | bytes 167772160 | tf_op jit(solution)/shard_map/all_to_all | solution.py:40
  2914.2 13.8 slice.98
  2928.0 22.9 slice.102
  2950.8 33.5 slice.106
  2984.3 44.3 %slice.110 = bf16[4,1,256,4,8192]{2,4,3,1,0:T(8,128)(2,1)} slice(bf16[5,1,256,4,8192]{2,4,3,1,0:T(8,128)(2,1)} %bitcast.3), slice={[0:4], [0:1], [0:256], [0:4], [0:8192]} | slice | bytes 134217728 | tf_op jit(solution)/shard_map/slice | solution.py:20
  3028.6 135.6 %copy.12 = bf16[5,1,256,4,8192]{4,3,2,0,1:T(4,128)(2,1)} copy(bf16[5,1,256,4,8192]{2,4,3,1,0:T(8,128)(2,1)} %bitcast.3) | data formatting | bytes 167772160 | tf_op jit(solution)/shard_map/all_to_all | solution.py:40
  3164.1 55.0 %copy.9 = bf16[2,1,256,4,8192]{4,3,2,0,1:T(4,128)(2,1)} copy(bf16[2,1,256,4,8192]{2,4,3,1,0:T(8,128)(2,1)} %slice.102) | data formatting | bytes 67108864 | tf_op jit(solution)/shard_map/slice | solution.py:20
  3219.1 29.2 copy.13
  3248.3 81.9 %copy.10 = bf16[3,1,256,4,8192]{4,3,2,0,1:T(4,128)(2,1)} copy(bf16[3,1,256,4,8192]{2,4,3,1,0:T(8,128)(2,1)} %slice.106) | data formatting | bytes 100663296 | tf_op jit(solution)/shard_map/slice | solution.py:20
  3330.2 42.4 %copy.14 = bf16[96,8,4,8192]{3,1,2,0:T(8,128)(2,1)} copy(bf16[96,8,4,8192]{3,2,1,0:T(4,128)(2,1)} %bitcast.32) | data formatting | bytes 100663296
  3372.5 108.7 %copy.11 = bf16[4,1,256,4,8192]{4,3,2,0,1:T(4,128)(2,1)} copy(bf16[4,1,256,4,8192]{2,4,3,1,0:T(8,128)(2,1)} %slice.110) | data formatting | bytes 134217728 | tf_op jit(solution)/shard_map/slice | solution.py:20
  3481.2 55.5 %copy.15 = bf16[128,8,4,8192]{3,1,2,0:T(8,128)(2,1)} copy(bf16[128,8,4,8192]{3,2,1,0:T(4,128)(2,1)} %bitcast.16) | data formatting | bytes 134217728
  3536.7 68.8 %copy.16 = bf16[160,8,4,8192]{3,1,2,0:T(8,128)(2,1)} copy(bf16[160,8,4,8192]{3,2,1,0:T(4,128)(2,1)} %bitcast.20) | data formatting | bytes 167772160
  3605.6 0.0 all-gather.3.cloned.1.call-done
  3605.6 0.0 copy-done.11
  3605.6 0.0 copy-done.15
  3605.6 0.0 copy-start.14
  3605.6 15.0 fusion.83
  3620.6 0.9 pad_dynamic-update-slice_fusion.7
  3621.5 0.0 copy-done.14
  3621.5 15.0 fusion.80
  3636.6 0.9 pad_dynamic-update-slice_fusion.6
  3637.4 0.0 copy-done.4
  3637.5 0.0 copy-done.13
  3637.5 18.8 fusion.71
  3656.3 0.9 pad_dynamic-update-slice_fusion.5
  3657.2 0.0 copy-done.12
  3657.2 19.0 fusion.68
  3676.2 0.9 pad_dynamic-update-slice_fusion.4
  3677.1 0.0 copy-done.3
  3677.1 0.0 copy-done.10
  3677.1 23.6 fusion.59
  3700.7 0.9 pad_dynamic-update-slice_fusion.3
  3701.6 0.0 copy-done.9
  3701.6 23.6 fusion.56
  3725.2 0.9 pad_dynamic-update-slice_fusion.2
  3726.1 0.0 copy-done.2
  3726.1 0.0 copy-done.8
  3726.1 29.1 fusion.47
  3755.1 0.9 pad_dynamic-update-slice_fusion.1
  3756.0 0.0 copy-done.7
  3756.0 29.1 fusion.44
  3785.1 0.9 pad_dynamic-update-slice_fusion
  3786.0 0.0 copy-done.1
  3786.0 35.8 fusion.35
  3821.8 35.6 fusion.29
  (18 shorter events, 0.0 us)
Async XLA Ops:
  6.5 955.9 %all-gather.5.cloned.1.call-start = ((), (), s32[]{:S(2)}) async-start(), calls=%async_computation.2 | async-start | bytes 125829120 | tf_op jit(solution)/shard_map/all_gather | solution.py:38
  7.3 3598.3 %all-gather.3.cloned.1.call-start = ((), (), s32[]{:S(2)}) async-start(), calls=%async_computation.1 | async-start | bytes 209715200 | tf_op jit(solution)/shard_map/all_gather | solution.py:37
  1017.8 1797.3 %all-to-all-start = ((bf16[5,4,256,8192]{3,2,0,1:T(8,128)(2,1)}), bf16[5,4,256,8192]{3,2,0,1:T(8,128)(2,1)}, u32[]{:S(2)}, u32[]{:S(2)}) async-start(bf16[5,4,256,8192]{3,2,0,1:T(8,128)(2,1)} %copy.7), calls=%async_computation | async-start | bytes 167772160 | tf_op jit(solution)/shard_map/all_to_all | solution.py:40
  1035.9 1.8 copy-start
  3536.7 68.9 %copy-start.11 = (s32[256]{0:T(256)S(1)}, s32[256]{0:T(256)}, u32[]{:S(2)}) copy-start(s32[256]{0:T(256)} %slice.96) | copy-start | bytes 3076
  3536.7 68.9 %copy-start.15 = (s32[256]{0:T(256)S(1)}, s32[256]{0:T(256)}, u32[]{:S(2)}) copy-start(s32[256]{0:T(256)} %get-tuple-element.5) | copy-start | bytes 3076
  3605.6 15.9 copy-start.14
  3621.5 15.9 copy-start.4
  3621.5 15.9 copy-start.13
  3637.5 19.7 copy-start.12
  3657.2 19.9 copy-start.3
  3657.2 19.9 copy-start.10
  3677.1 24.5 copy-start.9
  3701.6 24.5 copy-start.2
  3701.6 24.5 copy-start.8
  3726.1 30.0 copy-start.7
  3756.0 30.0 copy-start.1
  3756.0 30.0 copy-start.6
  3786.0 35.8 copy-start.5
Sparse Core Ops, SparseCore 0:
  8.8 953.5 all-gather.4
  963.9 1839.4 all-gather.2
where the time goes:
time: 3890 us; the launch traced here: 3860 us
  waiting for transfers between devices  2730 us (70%)
  local copies, waits for them, and re-layouts  855 us (22%)
  matrix products  245 us (6%)
    all_to_all x1, waiting for transfers between devices, local_fn(): swapped = lax.all_to_all(grouped, 'col', 1, 3, tiled=True)  1770 us
    all_gather x1, waiting for transfers between devices, local_fn(): lax.all_gather(a_local.reshape(local_rows // BLOCK, BLOCK, m_local), 'row...  954 us
    slice x7, local copies, waits for them, and re-layouts, lower_part(): col_panel[:col_width]  360 us
    dot_general x10, matrix products, lower_part(): lax.dot_general(row_panel[first_blk * BLOCK:last_blk * BLOCK], col_panel[...  245 us
    all_to_all x2, local copies, waits for them, and re-layouts, local_fn(): swapped = lax.all_to_all(grouped, 'col', 1, 3, tiled=True)  235 us
    unnamed x44, local copies, waits for them, and re-layouts  203 us
  transfers between devices with their start and end apart: 3, of which 2 were waited for; matrix products, arithmetic and copies ran while one was open for 22% of the time, Pallas kernels for 0%

commit v1 on v0

v1 whole, which is shorter than its diff:
```python
import functools

import jax
import jax.numpy as jnp
from jax import lax
from jax.experimental import pallas as pl
from jax.experimental.pallas import tpu as pltpu
from jax.sharding import PartitionSpec as P

BLOCK = 256
RING = 3
MESH = pl.DeviceIdType.MESH
DIMS = (((1,), (1,)), ((), ()))


def dot_t(lhs, rhs):
    return lax.dot_general(lhs, rhs, DIMS, preferred_element_type=jnp.float32)


def loop(lower, upper, body):
    def step(i, carry):
        body(i)
        return carry

    lax.fori_loop(lower, upper, step, 0)


def kernel(a, out, got_a, got_core, got_x, got_y, kept, ready, own, part, other, cols, rows,
           load_sem, send_a, recv_a, send_core, recv_core, send_x, recv_x, send_y, recv_y):
    nb = a.shape[0]
    cb = nb // 2
    half = a.shape[2] // 2
    y = lax.axis_index("row")
    c = lax.axis_index("col")
    x = lax.div(c, 2)
    k = lax.rem(c, 2)
    same = k == y
    core_dev = {"col": 2 * x + 1 - k}
    x_dev = {"col": 2 * (1 - x) + k}
    y_dev = {"row": 1 - y}

    barrier = pltpu.get_barrier_semaphore()
    for dev in (core_dev, x_dev, y_dev):
        pl.semaphore_signal(barrier, inc=1, device_id=dev, device_id_type=MESH)
    pl.semaphore_wait(barrier, 3)

    def remote(src, dst, send, recv, dev):
        return pltpu.make_async_remote_copy(src_ref=src, dst_ref=dst, send_sem=send, recv_sem=recv,
                                            device_id=dev, device_id_type=MESH)

    def fetch(src, dst, sem=0):
        copy = pltpu.make_async_copy(src, dst, load_sem.at[sem])
        copy.start()
        return copy

    def a_copy(b):
        return remote(a.at[b, :, pl.ds(pl.multiple_of((1 - y) * half, half), half)], got_a.at[b],
                      send_a.at[b], recv_a.at[b], y_dev)

    loop(0, nb, lambda b: a_copy(b).start())
    first = fetch(a.at[:, :, pl.ds(pl.multiple_of(y * half, half), half)], own.at[pl.ds(0, nb)], 0)
    second = fetch(a.at[:, :, pl.ds(pl.multiple_of((1 - y) * half, half), half)], own.at[pl.ds(nb, nb)], 1)

    def core_copy(job):
        slot = lax.rem(job, RING)
        return remote(part.at[slot], got_core.at[job], send_core.at[slot], recv_core.at[job], core_dev)

    def x_copy(job, i):
        slot = lax.rem(job, RING)
        return remote(part.at[slot, i], got_x.at[job, i], send_x.at[slot, i], recv_x.at[job, i], x_dev)

    def y_copy(b, i):
        s = lax.div(i, 2)
        return remote(ready.at[b, i], got_y.at[b, s], send_y.at[b, s], recv_y.at[b, s], y_dev)

    def add_other(slot, lower, upper):
        def one(i):
            part[slot, i] = part[slot, i] + other[i]

        loop(lower, upper, one)

    def same_send(lo):
        return jnp.logical_and(same, lax.rem(lo, 2) != x)

    def same_recv(lo):
        return jnp.logical_and(same, lax.rem(lo, 2) == x)

    def same_drain(lo):
        @pl.when(jnp.logical_not(same))
        def _():
            core_copy(lo).wait_send()

        @pl.when(same_send(lo))
        def _():
            loop(lo, nb, lambda i: x_copy(lo, i).wait_send())

    def same_compute(lo):
        slot = lax.rem(lo, RING)

        @pl.when(lo >= RING)
        def _():
            same_drain(lo - RING)

        def one(i):
            part[slot, i] = dot_t(own[i], own[lo]) + dot_t(own[nb + i], own[nb + lo])

        loop(lo, nb, one)

        @pl.when(jnp.logical_not(same))
        def _():
            core_copy(lo).start()

    def same_reduce(lo):
        slot = lax.rem(lo, RING)

        @pl.when(same)
        def _():
            core_copy(lo).wait_recv()
            fetch(got_core.at[lo], other).wait()
            add_other(slot, lo, nb)

        @pl.when(same_send(lo))
        def _():
            loop(lo, nb, lambda i: x_copy(lo, i).start())

    def same_final(lo):
        slot = lax.rem(lo, RING)

        @pl.when(same_recv(lo))
        def _():
            loop(lo, nb, lambda i: x_copy(lo, i).wait_recv())
            fetch(got_x.at[lo], other).wait()
            above = (lax.broadcasted_iota(jnp.int32, (BLOCK, BLOCK), 0)
                     < lax.broadcasted_iota(jnp.int32, (BLOCK, BLOCK), 1))

            def one(i):
                drop = jnp.logical_or(i < lo, jnp.logical_and(i == lo, above))
                cols[pl.ds(pl.multiple_of(i * BLOCK, BLOCK), BLOCK), :] = jnp.where(
                    drop, 0.0, part[slot, i] + other[i]).astype(cols.dtype)

            loop(0, nb, one)
            s = lax.div(lo, 2)
            fetch(cols, out.at[:, pl.ds(pl.multiple_of(s * BLOCK, BLOCK), BLOCK)]).wait()

    first.wait()
    second.wait()

    def same_step(t):
        @pl.when(t < nb)
        def _():
            same_compute(t)

        @pl.when(jnp.logical_and(t >= 1, t <= nb))
        def _():
            same_reduce(t - 1)

        @pl.when(t >= 2)
        def _():
            same_final(t - 2)

    loop(0, nb + 2, same_step)

    def mixed_send(b, i):
        split = b + 1 - y
        stay = jnp.logical_and(jnp.logical_not(same), jnp.logical_and(i >= split, lax.rem(b, 2) != x))
        cross = jnp.logical_and(same, jnp.logical_and(i < split, lax.rem(i, 2) != x))
        return jnp.logical_or(stay, cross)

    def mixed_recv(b, i):
        split = b + 1 - y
        stay = jnp.logical_and(jnp.logical_not(same), jnp.logical_and(i >= split, lax.rem(b, 2) == x))
        cross = jnp.logical_and(same, jnp.logical_and(i < split, lax.rem(i, 2) == x))
        return jnp.logical_or(stay, cross)

    def each(cond, action):
        def one(i):
            @pl.when(cond(i))
            def _():
                action(i)

        loop(0, nb, one)

    def mixed_drain(b):
        each(lambda i: mixed_send(b, i), lambda i: x_copy(nb + b, i).wait_send())

    def mixed_step(b):
        job = nb + b
        slot = lax.rem(job, RING)
        split = b + 1 - y

        @pl.when(b < RING)
        def _():
            same_drain(job - RING)

        @pl.when(b >= RING)
        def _():
            mixed_drain(b - RING)

        a_copy(b).wait_recv()
        fetch(got_a.at[b], own.at[2 * nb]).wait()

        def one(i):
            lhs = jnp.where(i >= split, i, 2 * nb)
            rhs = jnp.where(i >= split, 2 * nb, i)
            part[slot, i] = dot_t(own[lhs], own[rhs])

        loop(0, nb, one)
        swap = core_copy(job)
        swap.start()
        swap.wait_recv()
        load = fetch(got_core.at[job], other)
        swap.wait_send()
        load.wait()
        add_other(slot, 0, nb)

        each(lambda i: mixed_send(b, i), lambda i: x_copy(job, i).start())
        each(lambda i: mixed_recv(b, i), lambda i: x_copy(job, i).wait_recv())
        fetch(got_x.at[job], other).wait()

        @pl.when(jnp.logical_and(jnp.logical_not(same), lax.rem(b, 2) == x))
        def _():
            add_other(slot, split, nb)
            fetch(part.at[slot], kept.at[:, lax.div(b, 2)]).wait()

        @pl.when(same)
        def _():
            def add(i):
                part[slot, i] = part[slot, i] + other[i]

            each(lambda i: mixed_recv(b, i), add)
            fetch(part.at[slot], ready.at[b]).wait()
            each(lambda i: mixed_recv(b, i), lambda i: y_copy(b, i).start())

    loop(0, nb, mixed_step)

    @pl.when(jnp.logical_not(same))
    def _():
        def final(hi):
            def wait_one(s):
                i = 2 * s + x

                @pl.when(i < hi + y)
                def _():
                    remote(ready.at[hi, i], got_y.at[hi, s], send_y.at[hi, s], recv_y.at[hi, s], y_dev).wait_recv()

            loop(0, cb, wait_one)
            mine = fetch(kept.at[hi], other.at[pl.ds(0, cb)], 0)
            theirs = fetch(got_y.at[hi], other.at[pl.ds(cb, cb)], 1)
            mine.wait()
            theirs.wait()
            for s in range(cb):
                rows[:, s * BLOCK:(s + 1) * BLOCK] = jnp.where(
                    2 * s + x < hi + y, other[s] + other[cb + s], 0.0).astype(rows.dtype)
            fetch(rows, out.at[pl.ds(pl.multiple_of(hi * BLOCK, BLOCK), BLOCK), :]).wait()

        loop(0, nb, final)

    def finish(b):
        @pl.when(b >= nb - RING)
        def _():
            mixed_drain(b)

        @pl.when(same)
        def _():
            each(lambda i: mixed_recv(b, i), lambda i: y_copy(b, i).wait_send())

        a_copy(b).wait_send()

    loop(0, nb, finish)


def solution(mesh):
    def local_fn(a_local):
        local_rows, m_local = a_local.shape
        nb = local_rows // BLOCK
        cb = nb // 2
        half = m_local // 2
        f32, bf16 = jnp.float32, a_local.dtype
        hbm = pl.BlockSpec(memory_space=pl.ANY)
        shapes = [
            jax.ShapeDtypeStruct((local_rows, cb * BLOCK), bf16),
            jax.ShapeDtypeStruct((nb, BLOCK, half), bf16),
            jax.ShapeDtypeStruct((2 * nb, nb, BLOCK, BLOCK), f32),
            jax.ShapeDtypeStruct((2 * nb, nb, BLOCK, BLOCK), f32),
            jax.ShapeDtypeStruct((nb, cb, BLOCK, BLOCK), f32),
            jax.ShapeDtypeStruct((nb, cb, BLOCK, BLOCK), f32),
            jax.ShapeDtypeStruct((nb, nb, BLOCK, BLOCK), f32),
        ]
        dma = pltpu.SemaphoreType.DMA
        outs = pl.pallas_call(
            kernel,
            out_shape=shapes,
            in_specs=[hbm],
            out_specs=[hbm] * len(shapes),
            scratch_shapes=[
                pltpu.VMEM((2 * nb + 1, BLOCK, half), bf16),
                pltpu.VMEM((RING, nb, BLOCK, BLOCK), f32),
                pltpu.VMEM((nb, BLOCK, BLOCK), f32),
                pltpu.VMEM((local_rows, BLOCK), bf16),
                pltpu.VMEM((BLOCK, cb * BLOCK), bf16),
                dma((2,)),
                dma((nb,)), dma((nb,)),
                dma((RING,)), dma((2 * nb,)),
                dma((RING, nb)), dma((2 * nb, nb)),
                dma((nb, cb)), dma((nb, cb)),
            ],
            compiler_params=pltpu.CompilerParams(collective_id=0, has_side_effects=True,
                                                 vmem_limit_bytes=67043328),
            cost_estimate=pl.CostEstimate(flops=210 * 2 * BLOCK * BLOCK * half, bytes_accessed=400 * 2**20,
                                          transcendentals=0),
        )(a_local.reshape(nb, BLOCK, m_local))
        return outs[0]

    part_spec = P(("batch", "row"), "col")
    return jax.shard_map(local_fn, mesh=mesh, in_specs=(part_spec,), out_specs=part_spec, check_vma=False)
```

time: 3890 us -> 626 us (0.16)
  waiting for transfers between devices: 2730 us -> 0 us
  local copies, waits for them, and re-layouts: 855 us -> 6.07 us
  Pallas kernels: 0 us -> 608 us
  matrix products: 245 us -> 0 us
    all_to_all x1 -> x0, waiting for transfers between devices: 1770 us -> none  [local_fn(): swapped = lax.all_to_all(grouped, 'col', 1, 3, tiled=True)]
    all_gather x2 -> x0, waiting for transfers between devices: 954 us -> none  [the longest x1 954 us: local_fn(): lax.all_gather(a_local.reshape(local_rows // BLOCK, BLOCK, m_local), 'row...]
    pallas_call x0 -> x1, Pallas kernels: none -> 608 us  [local_fn(): pl.pallas_call(kernel, out_shape=shapes, in_specs=[hbm], out_specs=[hbm]...]
    slice x11 -> x0, local copies, waits for them, and re-layouts: 362 us -> none  [the longest x7 360 us: lower_part(): col_panel[:col_width]]
    dot_general x10 -> x0, matrix products: 245 us -> none  [lower_part(): lax.dot_general(row_panel[first_blk * BLOCK:last_blk * BLOCK], col_panel[...]
    all_to_all x2 -> x0, local copies, waits for them, and re-layouts: 235 us -> none  [local_fn(): swapped = lax.all_to_all(grouped, 'col', 1, 3, tiled=True)]
    unnamed x44 -> x1, local copies, waits for them, and re-layouts: 203 us -> 6.07 us
    reshape x1 -> x0, local copies, waits for them, and re-layouts: 55.4 us -> none  [local_fn(): gathered.reshape(n_total // (BLOCK * col_count), col_count, BLOCK, m_local)]
  transfers between devices with their start and end apart: 3 -> 0, of which waited for: 2 -> 0; matrix products, arithmetic and copies ran while one was open for 22% -> 0% of each run, Pallas kernels for 0% -> 0%
where the time goes in v1:
time: 626 us; the launch traced here: 614 us
  Pallas kernels  608 us (97%)
    pallas_call x1, Pallas kernels, local_fn(): pl.pallas_call(kernel, out_shape=shapes, in_specs=[hbm], out_specs=[hbm]...  608 us

profile of v1, /device:TPU:1, one launch (start us, length us, event | category | flops | bytes accessed | tf_op | source)
XLA Modules:
  0.0 614.1 jit_solution(2011004954679646500)
XLA Ops:
  0.0 608.1 %shard_map.17 = (bf16[2560,1280]{1,0:T(8,128)(2,1)}, bf16[10,256,4096]{2,1,0:T(8,128)(2,1)}, f32[20,10,256,256]{3,2,1,0:T(8,128)}, f32[20,10,256,256]{3,2,1,0:T(...) custom-call(bf16[10,256,8192]{2,1,0:T(8,128)(2,1)} %bitcast.1), custom_call_target="tpu_custom_call" | custom-call | flops 112742891520 | bytes 419430400 | tf_op jit(solution)/shard_map/pallas_call | solution.py:290
  608.1 6.1 copy.3

commit v2 on v1

--- a/solution.py
+++ b/solution.py
@@ -183,6 +183,27 @@
     def mixed_drain(b):
         each(lambda i: mixed_send(b, i), lambda i: x_copy(nb + b, i).wait_send())
 
+    def mixed_reduce(b):
+        job = nb + b
+        slot = lax.rem(job, RING)
+        split = b + 1 - y
+        each(lambda i: mixed_recv(b, i), lambda i: x_copy(job, i).wait_recv())
+        fetch(got_x.at[job], other).wait()
+
+        @pl.when(jnp.logical_and(jnp.logical_not(same), lax.rem(b, 2) == x))
+        def _():
+            add_other(slot, split, nb)
+            fetch(part.at[slot], kept.at[:, lax.div(b, 2)]).wait()
+
+        @pl.when(same)
+        def _():
+            def add(i):
+                part[slot, i] = part[slot, i] + other[i]
+
+            each(lambda i: mixed_recv(b, i), add)
+            fetch(part.at[slot], ready.at[b]).wait()
+            each(lambda i: mixed_recv(b, i), lambda i: y_copy(b, i).start())
+
     def mixed_step(b):
         job = nb + b
         slot = lax.rem(job, RING)
@@ -205,33 +226,22 @@
             part[slot, i] = dot_t(own[lhs], own[rhs])
 
         loop(0, nb, one)
+        core_copy(job).start()
+
+        @pl.when(b >= 1)
+        def _():
+            mixed_reduce(b - 1)
+
         swap = core_copy(job)
-        swap.start()
         swap.wait_recv()
         load = fetch(got_core.at[job], other)
         swap.wait_send()
         load.wait()
         add_other(slot, 0, nb)
-
         each(lambda i: mixed_send(b, i), lambda i: x_copy(job, i).start())
-        each(lambda i: mixed_recv(b, i), lambda i: x_copy(job, i).wait_recv())
-        fetch(got_x.at[job], other).wait()
-
-        @pl.when(jnp.logical_and(jnp.logical_not(same), lax.rem(b, 2) == x))
-        def _():
-            add_other(slot, split, nb)
-            fetch(part.at[slot], kept.at[:, lax.div(b, 2)]).wait()
-
-        @pl.when(same)
-        def _():
-            def add(i):
-                part[slot, i] = part[slot, i] + other[i]
-
-            each(lambda i: mixed_recv(b, i), add)
-            fetch(part.at[slot], ready.at[b]).wait()
-            each(lambda i: mixed_recv(b, i), lambda i: y_copy(b, i).start())
 
     loop(0, nb, mixed_step)
+    mixed_reduce(jnp.int32(nb - 1))
 
     @pl.when(jnp.logical_not(same))
     def _():

time: 626 us -> 550 us (0.88)
  the two profiles are of different devices: /device:TPU:1 before, /device:TPU:4 now
where the time goes in v2:
time: 550 us; the launch traced here: 549 us
  Pallas kernels  543 us (99%)
  local copies, waits for them, and re-layouts  6.07 us (1%)
    pallas_call x1, Pallas kernels, local_fn(): pl.pallas_call(kernel, out_shape=shapes, in_specs=[hbm], out_specs=[hbm]...  543 us

profile of v2, /device:TPU:4, one launch (start us, length us, event | category | flops | bytes accessed | tf_op | source)
XLA Modules:
  0.0 548.7 jit_solution(9543237384160520520)
XLA Ops:
  0.0 542.6 %shard_map.17 = (bf16[2560,1280]{1,0:T(8,128)(2,1)}, bf16[10,256,4096]{2,1,0:T(8,128)(2,1)}, f32[20,10,256,256]{3,2,1,0:T(8,128)}, f32[20,10,256,256]{3,2,1,0:T(...) custom-call(bf16[10,256,8192]{2,1,0:T(8,128)(2,1)} %bitcast.1), custom_call_target="tpu_custom_call" | custom-call | flops 112742891520 | bytes 419430400 | tf_op jit(solution)/shard_map/pallas_call | solution.py:300
  542.6 6.1 %copy.3 = bf16[2560,1280]{1,0:T(8,128)(2,1)} copy(bf16[2560,1280]{1,0:T(8,128)(2,1)} %get-tuple-element.6) | data formatting | bytes 13107200

commit v3 on v2

--- a/solution.py
+++ b/solution.py
@@ -9,6 +9,8 @@
 
 BLOCK = 256
 RING = 3
+LANES = 128
+AHEAD = 2
 MESH = pl.DeviceIdType.MESH
 DIMS = (((1,), (1,)), ((), ()))
 
@@ -25,8 +27,8 @@
     lax.fori_loop(lower, upper, step, 0)
 
 
-def kernel(a, out, got_a, got_core, got_x, got_y, kept, ready, own, part, other, cols, rows,
-           load_sem, send_a, recv_a, send_core, recv_core, send_x, recv_x, send_y, recv_y):
+def kernel(a, out, got_a, got_core, got_x, got_y, kept, ready, moved, relayed, own, part, other, cols, rows, extra,
+           load_sem, send_a, recv_a, send_core, recv_core, send_x, recv_x, send_y, recv_y, send_m, recv_m):
     nb = a.shape[0]
     cb = nb // 2
     half = a.shape[2] // 2
@@ -53,11 +55,39 @@
         copy.start()
         return copy
 
-    def a_copy(b):
+    narrow_send = jnp.logical_and(x == 0, y == 0)
+    narrow_recv = jnp.logical_and(x == 0, y == 1)
+    takes_moved = jnp.logical_and(x == 1, y == 0)
+    relays = jnp.logical_and(x == 1, y == 1)
+
+    def wide_copy(b):
         return remote(a.at[b, :, pl.ds(pl.multiple_of((1 - y) * half, half), half)], got_a.at[b],
                       send_a.at[b], recv_a.at[b], y_dev)
 
-    loop(0, nb, lambda b: a_copy(b).start())
+    def narrow_copy(b):
+        return remote(a.at[b, :, pl.ds(half + LANES, half - LANES)], got_a.at[b, :, pl.ds(LANES, half - LANES)],
+                      send_a.at[b], recv_a.at[b], y_dev)
+
+    def a_copy(b, narrow, action):
+        @pl.when(narrow)
+        def _():
+            action(narrow_copy(b))
+
+        @pl.when(jnp.logical_not(narrow))
+        def _():
+            action(wide_copy(b))
+
+    def start_a(b):
+        a_copy(b, narrow_send, lambda copy: copy.start())
+
+    move = remote(a.at[:, :, pl.ds(half, LANES)], moved, send_m.at[0], recv_m.at[0], x_dev)
+    relay = remote(moved, relayed, send_m.at[1], recv_m.at[1], y_dev)
+
+    @pl.when(x == 0)
+    def _():
+        move.start()
+
+    loop(0, AHEAD, start_a)
     first = fetch(a.at[:, :, pl.ds(pl.multiple_of(y * half, half), half)], own.at[pl.ds(0, nb)], 0)
     second = fetch(a.at[:, :, pl.ds(pl.multiple_of((1 - y) * half, half), half)], own.at[pl.ds(nb, nb)], 1)
 
@@ -144,6 +174,16 @@
 
     first.wait()
     second.wait()
+
+    @pl.when(x == 1)
+    def _():
+        move.wait_recv()
+
+    @pl.when(relays)
+    def _():
+        relay.start()
+
+    loop(AHEAD, nb, start_a)
 
     def same_step(t):
         @pl.when(t < nb)
@@ -204,6 +244,16 @@
             fetch(part.at[slot], ready.at[b]).wait()
             each(lambda i: mixed_recv(b, i), lambda i: y_copy(b, i).start())
 
+    @pl.when(narrow_recv)
+    def _():
+        own[2 * nb, :, 0:LANES] = jnp.zeros((BLOCK, LANES), own.dtype)
+
+    @pl.when(takes_moved)
+    def _():
+        relay.wait_recv()
+        fetch(moved, extra.at[0]).wait()
+        fetch(relayed, extra.at[1]).wait()
+
     def mixed_step(b):
         job = nb + b
         slot = lax.rem(job, RING)
@@ -217,15 +267,32 @@
         def _():
             mixed_drain(b - RING)
 
-        a_copy(b).wait_recv()
-        fetch(got_a.at[b], own.at[2 * nb]).wait()
+        a_copy(b, narrow_recv, lambda copy: copy.wait_recv())
+
+        @pl.when(narrow_recv)
+        def _():
+            fetch(got_a.at[b, :, pl.ds(LANES, half - LANES)], own.at[2 * nb, :, pl.ds(LANES, half - LANES)]).wait()
+
+        @pl.when(jnp.logical_not(narrow_recv))
+        def _():
+            fetch(got_a.at[b], own.at[2 * nb]).wait()
 
         def one(i):
             lhs = jnp.where(i >= split, i, 2 * nb)
             rhs = jnp.where(i >= split, 2 * nb, i)
             part[slot, i] = dot_t(own[lhs], own[rhs])
 
+        def one_extra(i):
+            left = jnp.where(i >= split, 0, 1)
+            part[slot, i] = part[slot, i] + dot_t(extra[left, jnp.where(i >= split, i, b)],
+                                                  extra[1 - left, jnp.where(i >= split, b, i)])
+
         loop(0, nb, one)
+
+        @pl.when(takes_moved)
+        def _():
+            loop(0, nb, one_extra)
+
         core_copy(job).start()
 
         @pl.when(b >= 1)
@@ -274,9 +341,17 @@
         def _():
             each(lambda i: mixed_recv(b, i), lambda i: y_copy(b, i).wait_send())
 
-        a_copy(b).wait_send()
+        a_copy(b, narrow_send, lambda copy: copy.wait_send())
 
     loop(0, nb, finish)
+
+    @pl.when(x == 0)
+    def _():
+        move.wait_send()
+
+    @pl.when(relays)
+    def _():
+        relay.wait_send()
 
 
 def solution(mesh):
@@ -295,6 +370,8 @@
             jax.ShapeDtypeStruct((nb, cb, BLOCK, BLOCK), f32),
             jax.ShapeDtypeStruct((nb, cb, BLOCK, BLOCK), f32),
             jax.ShapeDtypeStruct((nb, nb, BLOCK, BLOCK), f32),
+            jax.ShapeDtypeStruct((nb, BLOCK, LANES), bf16),
+            jax.ShapeDtypeStruct((nb, BLOCK, LANES), bf16),
         ]
         dma = pltpu.SemaphoreType.DMA
         outs = pl.pallas_call(
@@ -308,11 +385,13 @@
                 pltpu.VMEM((nb, BLOCK, BLOCK), f32),
                 pltpu.VMEM((local_rows, BLOCK), bf16),
                 pltpu.VMEM((BLOCK, cb * BLOCK), bf16),
+                pltpu.VMEM((2, nb, BLOCK, LANES), bf16),
                 dma((2,)),
                 dma((nb,)), dma((nb,)),
                 dma((RING,)), dma((2 * nb,)),
                 dma((RING, nb)), dma((2 * nb, nb)),
                 dma((nb, cb)), dma((nb, cb)),
+                dma((2,)), dma((2,)),
             ],
             compiler_params=pltpu.CompilerParams(collective_id=0, has_side_effects=True,
                                                  vmem_limit_bytes=67043328),

time: 550 us -> 538 us (0.978)
  the two profiles are of different devices: /device:TPU:4 before, /device:TPU:1 now
where the time goes in v3:
time: 538 us; the launch traced here: 536 us
  Pallas kernels  530 us (99%)
  local copies, waits for them, and re-layouts  6.07 us (1%)
    pallas_call x1, Pallas kernels, local_fn(): pl.pallas_call(kernel, out_shape=shapes, in_specs=[hbm], out_specs=[hbm]...  530 us

profile of v3, /device:TPU:1, one launch (start us, length us, event | category | flops | bytes accessed | tf_op | source)
XLA Modules:
  0.0 536.5 jit_solution(6604665748547239214)
XLA Ops:
  0.0 530.4 %shard_map.17 = (bf16[2560,1280]{1,0:T(8,128)(2,1)}, bf16[10,256,4096]{2,1,0:T(8,128)(2,1)}, f32[20,10,256,256]{3,2,1,0:T(8,128)}, f32[20,10,256,256]{3,2,1,0:T(...) custom-call(bf16[10,256,8192]{2,1,0:T(8,128)(2,1)} %bitcast.1), custom_call_target="tpu_custom_call" | custom-call | flops 112742891520 | bytes 419430400 | tf_op jit(solution)/shard_map/pallas_call | solution.py:377
  530.4 6.1 %copy.3 = bf16[2560,1280]{1,0:T(8,128)(2,1)} copy(bf16[2560,1280]{1,0:T(8,128)(2,1)} %get-tuple-element.6) | data formatting | bytes 13107200

commit v4 on v3

--- a/solution.py
+++ b/solution.py
@@ -27,8 +27,8 @@
     lax.fori_loop(lower, upper, step, 0)
 
 
-def kernel(a, out, got_a, got_core, got_x, got_y, kept, ready, moved, relayed, own, part, other, cols, rows, extra,
-           load_sem, send_a, recv_a, send_core, recv_core, send_x, recv_x, send_y, recv_y, send_m, recv_m):
+def kernel(a, out, got_a, got_core, got_x, got_y, kept, ready, moved, relayed, own, part, other, cols, rows, extra, last_y,
+           load_sem, far_sem, send_a, recv_a, send_core, recv_core, send_x, recv_x, send_y, recv_y, send_m, recv_m):
     nb = a.shape[0]
     cb = nb // 2
     half = a.shape[2] // 2
@@ -88,8 +88,17 @@
         move.start()
 
     loop(0, AHEAD, start_a)
-    first = fetch(a.at[:, :, pl.ds(pl.multiple_of(y * half, half), half)], own.at[pl.ds(0, nb)], 0)
-    second = fetch(a.at[:, :, pl.ds(pl.multiple_of((1 - y) * half, half), half)], own.at[pl.ds(nb, nb)], 1)
+    first = fetch(a.at[:, :, pl.ds(pl.multiple_of(y * half, half), half)], own.at[pl.ds(0, nb)])
+
+    def far_slot(lo, i):
+        return nb + 1 + jnp.where(i == lo, lax.rem(lo, 2), 2 + lax.rem(i, 2))
+
+    def far_copy(lo, i):
+        slot = far_slot(lo, i)
+        return pltpu.make_async_copy(a.at[i, :, pl.ds(pl.multiple_of((1 - y) * half, half), half)], own.at[slot],
+                                     far_sem.at[slot - nb - 1])
+
+    far_copy(jnp.int32(0), jnp.int32(0)).start()
 
     def core_copy(job):
         slot = lax.rem(job, RING)
@@ -99,9 +108,16 @@
         slot = lax.rem(job, RING)
         return remote(part.at[slot, i], got_x.at[job, i], send_x.at[slot, i], recv_x.at[job, i], x_dev)
 
-    def y_copy(b, i):
+    def y_copy(b, i, action):
         s = lax.div(i, 2)
-        return remote(ready.at[b, i], got_y.at[b, s], send_y.at[b, s], recv_y.at[b, s], y_dev)
+
+        @pl.when(b < nb - 1)
+        def _():
+            action(remote(ready.at[b, i], got_y.at[b, s], send_y.at[b, s], recv_y.at[b, s], y_dev))
+
+        @pl.when(b == nb - 1)
+        def _():
+            action(remote(ready.at[b, i], last_y.at[s], send_y.at[b, s], recv_y.at[b, s], y_dev))
 
     def add_other(slot, lower, upper):
         def one(i):
@@ -132,7 +148,14 @@
             same_drain(lo - RING)
 
         def one(i):
-            part[slot, i] = dot_t(own[i], own[lo]) + dot_t(own[nb + i], own[nb + lo])
+            far_copy(lo, i).wait()
+            last = i == nb - 1
+
+            @pl.when(jnp.logical_or(jnp.logical_not(last), lo < nb - 1))
+            def _():
+                far_copy(jnp.where(last, lo + 1, lo), jnp.where(last, lo + 1, i + 1)).start()
+
+            part[slot, i] = dot_t(own[i], own[lo]) + dot_t(own[far_slot(lo, i)], own[far_slot(lo, lo)])
 
         loop(lo, nb, one)
 
@@ -173,7 +196,6 @@
             fetch(cols, out.at[:, pl.ds(pl.multiple_of(s * BLOCK, BLOCK), BLOCK)]).wait()
 
     first.wait()
-    second.wait()
 
     @pl.when(x == 1)
     def _():
@@ -242,11 +264,11 @@
 
             each(lambda i: mixed_recv(b, i), add)
             fetch(part.at[slot], ready.at[b]).wait()
-            each(lambda i: mixed_recv(b, i), lambda i: y_copy(b, i).start())
+            each(lambda i: mixed_recv(b, i), lambda i: y_copy(b, i, lambda copy: copy.start()))
 
     @pl.when(narrow_recv)
     def _():
-        own[2 * nb, :, 0:LANES] = jnp.zeros((BLOCK, LANES), own.dtype)
+        own[nb, :, 0:LANES] = jnp.zeros((BLOCK, LANES), own.dtype)
 
     @pl.when(takes_moved)
     def _():
@@ -271,15 +293,15 @@
 
         @pl.when(narrow_recv)
         def _():
-            fetch(got_a.at[b, :, pl.ds(LANES, half - LANES)], own.at[2 * nb, :, pl.ds(LANES, half - LANES)]).wait()
+            fetch(got_a.at[b, :, pl.ds(LANES, half - LANES)], own.at[nb, :, pl.ds(LANES, half - LANES)]).wait()
 
         @pl.when(jnp.logical_not(narrow_recv))
         def _():
-            fetch(got_a.at[b], own.at[2 * nb]).wait()
+            fetch(got_a.at[b], own.at[nb]).wait()
 
         def one(i):
-            lhs = jnp.where(i >= split, i, 2 * nb)
-            rhs = jnp.where(i >= split, 2 * nb, i)
+            lhs = jnp.where(i >= split, i, nb)
+            rhs = jnp.where(i >= split, nb, i)
             part[slot, i] = dot_t(own[lhs], own[rhs])
 
         def one_extra(i):
@@ -312,16 +334,14 @@
 
     @pl.when(jnp.logical_not(same))
     def _():
+        def wait_y(hi, s):
+            @pl.when(2 * s + x < hi + y)
+            def _():
+                y_copy(hi, 2 * s + x, lambda copy: copy.wait_recv())
+
         def final(hi):
-            def wait_one(s):
-                i = 2 * s + x
-
-                @pl.when(i < hi + y)
-                def _():
-                    remote(ready.at[hi, i], got_y.at[hi, s], send_y.at[hi, s], recv_y.at[hi, s], y_dev).wait_recv()
-
-            loop(0, cb, wait_one)
             mine = fetch(kept.at[hi], other.at[pl.ds(0, cb)], 0)
+            loop(0, cb, lambda s: wait_y(hi, s))
             theirs = fetch(got_y.at[hi], other.at[pl.ds(cb, cb)], 1)
             mine.wait()
             theirs.wait()
@@ -330,7 +350,16 @@
                     2 * s + x < hi + y, other[s] + other[cb + s], 0.0).astype(rows.dtype)
             fetch(rows, out.at[pl.ds(pl.multiple_of(hi * BLOCK, BLOCK), BLOCK), :]).wait()
 
-        loop(0, nb, final)
+        loop(0, nb - 1, final)
+        fetch(kept.at[nb - 1], other.at[pl.ds(0, cb)]).wait()
+        stores = []
+        for s in range(cb):
+            wait_y(nb - 1, s)
+            span = pl.ds(s * BLOCK, BLOCK)
+            rows[:, span] = jnp.where(2 * s + x < nb - 1 + y, other[s] + last_y[s], 0.0).astype(rows.dtype)
+            stores.append(fetch(rows.at[:, span], out.at[pl.ds((nb - 1) * BLOCK, BLOCK), span], s))
+        for store in stores:
+            store.wait()
 
     def finish(b):
         @pl.when(b >= nb - RING)
@@ -339,7 +368,7 @@
 
         @pl.when(same)
         def _():
-            each(lambda i: mixed_recv(b, i), lambda i: y_copy(b, i).wait_send())
+            each(lambda i: mixed_recv(b, i), lambda i: y_copy(b, i, lambda copy: copy.wait_send()))
 
         a_copy(b, narrow_send, lambda copy: copy.wait_send())
 
@@ -380,13 +409,14 @@
             in_specs=[hbm],
             out_specs=[hbm] * len(shapes),
             scratch_shapes=[
-                pltpu.VMEM((2 * nb + 1, BLOCK, half), bf16),
+                pltpu.VMEM((nb + 5, BLOCK, half), bf16),
                 pltpu.VMEM((RING, nb, BLOCK, BLOCK), f32),
                 pltpu.VMEM((nb, BLOCK, BLOCK), f32),
                 pltpu.VMEM((local_rows, BLOCK), bf16),
                 pltpu.VMEM((BLOCK, cb * BLOCK), bf16),
                 pltpu.VMEM((2, nb, BLOCK, LANES), bf16),
-                dma((2,)),
+                pltpu.VMEM((cb, BLOCK, BLOCK), f32),
+                dma((cb,)), dma((4,)),
                 dma((nb,)), dma((nb,)),
                 dma((RING,)), dma((2 * nb,)),
                 dma((RING, nb)), dma((2 * nb, nb)),
@@ -394,7 +424,7 @@
                 dma((2,)), dma((2,)),
             ],
             compiler_params=pltpu.CompilerParams(collective_id=0, has_side_effects=True,
-                                                 vmem_limit_bytes=67043328),
+                                                 vmem_limit_bytes=46 * 2**20),
             cost_estimate=pl.CostEstimate(flops=210 * 2 * BLOCK * BLOCK * half, bytes_accessed=400 * 2**20,
                                           transcendentals=0),
         )(a_local.reshape(nb, BLOCK, m_local))

time: 538 us -> 534 us (level)
  no operation moved by 1% of the time
where the time goes in v4:
time: 534 us; the launch traced here: 531 us
  Pallas kernels  528 us (99%)
    pallas_call x1, Pallas kernels, local_fn(): pl.pallas_call(kernel, out_shape=shapes, in_specs=[hbm], out_specs=[hbm]...  528 us

profile of v4, /device:TPU:1, one launch (start us, length us, event | category | flops | bytes accessed | tf_op | source)
XLA Modules:
  0.0 531.0 jit_solution(4883304669700790704)
XLA Ops:
  0.0 528.2 %shard_map.17 = (bf16[2560,1280]{1,0:T(8,128)(2,1)S(1)}, bf16[10,256,4096]{2,1,0:T(8,128)(2,1)}, f32[20,10,256,256]{3,2,1,0:T(8,128)}, f32[20,10,256,256]{3,2,1,...) custom-call(bf16[10,256,8192]{2,1,0:T(8,128)(2,1)} %bitcast.1), custom_call_target="tpu_custom_call" | custom-call | flops 112742891520 | bytes 419430400 | tf_op jit(solution)/shard_map/pallas_call | solution.py:406
  528.2 2.8 copy.3

commit v5 on v4

--- a/solution.py
+++ b/solution.py
@@ -100,9 +100,10 @@
 
     far_copy(jnp.int32(0), jnp.int32(0)).start()
 
-    def core_copy(job):
+    def core_copy(job, h):
         slot = lax.rem(job, RING)
-        return remote(part.at[slot], got_core.at[job], send_core.at[slot], recv_core.at[job], core_dev)
+        span = pl.ds(h * cb, cb)
+        return remote(part.at[slot, span], got_core.at[job, span], send_core.at[slot, h], recv_core.at[job, h], core_dev)
 
     def x_copy(job, i):
         slot = lax.rem(job, RING)
@@ -117,7 +118,7 @@
 
         @pl.when(b == nb - 1)
         def _():
-            action(remote(ready.at[b, i], last_y.at[s], send_y.at[b, s], recv_y.at[b, s], y_dev))
+            action(remote(part.at[(2 * nb - 1) % RING, i], last_y.at[s], send_y.at[b, s], recv_y.at[b, s], y_dev))
 
     def add_other(slot, lower, upper):
         def one(i):
@@ -134,7 +135,8 @@
     def same_drain(lo):
         @pl.when(jnp.logical_not(same))
         def _():
-            core_copy(lo).wait_send()
+            core_copy(lo, 0).wait_send()
+            core_copy(lo, 1).wait_send()
 
         @pl.when(same_send(lo))
         def _():
@@ -161,14 +163,16 @@
 
         @pl.when(jnp.logical_not(same))
         def _():
-            core_copy(lo).start()
+            core_copy(lo, 0).start()
+            core_copy(lo, 1).start()
 
     def same_reduce(lo):
         slot = lax.rem(lo, RING)
 
         @pl.when(same)
         def _():
-            core_copy(lo).wait_recv()
+            core_copy(lo, 0).wait_recv()
+            core_copy(lo, 1).wait_recv()
             fetch(got_core.at[lo], other).wait()
             add_other(slot, lo, nb)
 
@@ -234,13 +238,13 @@
         cross = jnp.logical_and(same, jnp.logical_and(i < split, lax.rem(i, 2) == x))
         return jnp.logical_or(stay, cross)
 
-    def each(cond, action):
+    def each(cond, action, lower=0, upper=nb):
         def one(i):
             @pl.when(cond(i))
             def _():
                 action(i)
 
-        loop(0, nb, one)
+        loop(lower, upper, one)
 
     def mixed_drain(b):
         each(lambda i: mixed_send(b, i), lambda i: x_copy(nb + b, i).wait_send())
@@ -263,7 +267,11 @@
                 part[slot, i] = part[slot, i] + other[i]
 
             each(lambda i: mixed_recv(b, i), add)
-            fetch(part.at[slot], ready.at[b]).wait()
+
+            @pl.when(b < nb - 1)
+            def _():
+                fetch(part.at[slot], ready.at[b]).wait()
+
             each(lambda i: mixed_recv(b, i), lambda i: y_copy(b, i, lambda copy: copy.start()))
 
     @pl.when(narrow_recv)
@@ -289,6 +297,12 @@
         def _():
             mixed_drain(b - RING)
 
+        early = jnp.logical_and(b >= 1, b <= cb)
+
+        @pl.when(b > cb)
+        def _():
+            mixed_reduce(b - 1)
+
         a_copy(b, narrow_recv, lambda copy: copy.wait_recv())
 
         @pl.when(narrow_recv)
@@ -309,28 +323,51 @@
             part[slot, i] = part[slot, i] + dot_t(extra[left, jnp.where(i >= split, i, b)],
                                                   extra[1 - left, jnp.where(i >= split, b, i)])
 
-        loop(0, nb, one)
-
-        @pl.when(takes_moved)
-        def _():
-            loop(0, nb, one_extra)
-
-        core_copy(job).start()
-
-        @pl.when(b >= 1)
+        def compute_half(h):
+            loop(h * cb, h * cb + cb, one)
+
+            @pl.when(takes_moved)
+            def _():
+                loop(h * cb, h * cb + cb, one_extra)
+
+            core_copy(job, h).start()
+
+        loop(0, 2, compute_half)
+
+        @pl.when(early)
         def _():
             mixed_reduce(b - 1)
 
-        swap = core_copy(job)
-        swap.wait_recv()
-        load = fetch(got_core.at[job], other)
-        swap.wait_send()
-        load.wait()
-        add_other(slot, 0, nb)
-        each(lambda i: mixed_send(b, i), lambda i: x_copy(job, i).start())
+        def reduce_half(h):
+            swap = core_copy(job, h)
+            swap.wait_recv()
+            load = fetch(got_core.at[job, pl.ds(h * cb, cb)], other.at[pl.ds(h * cb, cb)])
+            swap.wait_send()
+            load.wait()
+            add_other(slot, h * cb, h * cb + cb)
+            each(lambda i: mixed_send(b, i), lambda i: x_copy(job, i).start(), h * cb, h * cb + cb)
+
+        loop(0, 2, reduce_half)
 
     loop(0, nb, mixed_step)
     mixed_reduce(jnp.int32(nb - 1))
+
+    def finish(b):
+        @pl.when(b >= nb - RING)
+        def _():
+            mixed_drain(b)
+
+        a_copy(b, narrow_send, lambda copy: copy.wait_send())
+
+    loop(0, nb, finish)
+
+    @pl.when(x == 0)
+    def _():
+        move.wait_send()
+
+    @pl.when(relays)
+    def _():
+        relay.wait_send()
 
     @pl.when(jnp.logical_not(same))
     def _():
@@ -350,37 +387,24 @@
                     2 * s + x < hi + y, other[s] + other[cb + s], 0.0).astype(rows.dtype)
             fetch(rows, out.at[pl.ds(pl.multiple_of(hi * BLOCK, BLOCK), BLOCK), :]).wait()
 
+        last_kept = fetch(kept.at[nb - 1], part.at[0, pl.ds(0, cb)], 2)
         loop(0, nb - 1, final)
-        fetch(kept.at[nb - 1], other.at[pl.ds(0, cb)]).wait()
+        last_kept.wait()
         stores = []
         for s in range(cb):
             wait_y(nb - 1, s)
             span = pl.ds(s * BLOCK, BLOCK)
-            rows[:, span] = jnp.where(2 * s + x < nb - 1 + y, other[s] + last_y[s], 0.0).astype(rows.dtype)
+            rows[:, span] = jnp.where(2 * s + x < nb - 1 + y, part[0, s] + last_y[s], 0.0).astype(rows.dtype)
             stores.append(fetch(rows.at[:, span], out.at[pl.ds((nb - 1) * BLOCK, BLOCK), span], s))
         for store in stores:
             store.wait()
 
-    def finish(b):
-        @pl.when(b >= nb - RING)
-        def _():
-            mixed_drain(b)
-
-        @pl.when(same)
-        def _():
+    @pl.when(same)
+    def _():
+        def finish_y(b):
             each(lambda i: mixed_recv(b, i), lambda i: y_copy(b, i, lambda copy: copy.wait_send()))
 
-        a_copy(b, narrow_send, lambda copy: copy.wait_send())
-
-    loop(0, nb, finish)
-
-    @pl.when(x == 0)
-    def _():
-        move.wait_send()
-
-    @pl.when(relays)
-    def _():
-        relay.wait_send()
+        loop(0, nb, finish_y)
 
 
 def solution(mesh):
@@ -418,7 +442,7 @@
                 pltpu.VMEM((cb, BLOCK, BLOCK), f32),
                 dma((cb,)), dma((4,)),
                 dma((nb,)), dma((nb,)),
-                dma((RING,)), dma((2 * nb,)),
+                dma((RING, 2)), dma((2 * nb, 2)),
                 dma((RING, nb)), dma((2 * nb, nb)),
                 dma((nb, cb)), dma((nb, cb)),
                 dma((2,)), dma((2,)),

time: 534 us -> 534 us (level)
  no operation moved by 1% of the time
where the time goes in v5:
time: 534 us; the launch traced here: 530 us
  Pallas kernels  528 us (99%)
    pallas_call x1, Pallas kernels, local_fn(): pl.pallas_call(kernel, out_shape=shapes, in_specs=[hbm], out_specs=[hbm]...  528 us

profile of v5, /device:TPU:1, one launch (start us, length us, event | category | flops | bytes accessed | tf_op | source)
XLA Modules:
  0.0 530.4 jit_solution(14431317429789517463)
XLA Ops:
  0.0 527.6 %shard_map.17 = (bf16[2560,1280]{1,0:T(8,128)(2,1)S(1)}, bf16[10,256,4096]{2,1,0:T(8,128)(2,1)}, f32[20,10,256,256]{3,2,1,0:T(8,128)}, f32[20,10,256,256]{3,2,1,...) custom-call(bf16[10,256,8192]{2,1,0:T(8,128)(2,1)} %bitcast.1), custom_call_target="tpu_custom_call" | custom-call | flops 112742891520 | bytes 419430400 | tf_op jit(solution)/shard_map/pallas_call | solution.py:430
  527.6 2.8 copy.3

commit v6 on v5

--- a/solution.py
+++ b/solution.py
@@ -350,7 +350,9 @@
         loop(0, 2, reduce_half)
 
     loop(0, nb, mixed_step)
-    mixed_reduce(jnp.int32(nb - 1))
+    @pl.when(same)
+    def _():
+        mixed_reduce(jnp.int32(nb - 1))
 
     def finish(b):
         @pl.when(b >= nb - RING)
@@ -387,9 +389,9 @@
                     2 * s + x < hi + y, other[s] + other[cb + s], 0.0).astype(rows.dtype)
             fetch(rows, out.at[pl.ds(pl.multiple_of(hi * BLOCK, BLOCK), BLOCK), :]).wait()
 
-        last_kept = fetch(kept.at[nb - 1], part.at[0, pl.ds(0, cb)], 2)
         loop(0, nb - 1, final)
-        last_kept.wait()
+        mixed_reduce(jnp.int32(nb - 1))
+        fetch(kept.at[nb - 1], part.at[0, pl.ds(0, cb)]).wait()
         stores = []
         for s in range(cb):
             wait_y(nb - 1, s)

time: 534 us -> 534 us (level)
  no operation moved by 1% of the time
where the time goes in v6:
time: 534 us; the launch traced here: 530 us
  Pallas kernels  528 us (99%)
    pallas_call x1, Pallas kernels, local_fn(): pl.pallas_call(kernel, out_shape=shapes, in_specs=[hbm], out_specs=[hbm]...  528 us

profile of v6, /device:TPU:1, one launch (start us, length us, event | category | flops | bytes accessed | tf_op | source)
XLA Modules:
  0.0 530.4 jit_solution(10628290728344078509)
XLA Ops:
  0.0 527.6 %shard_map.17 = (bf16[2560,1280]{1,0:T(8,128)(2,1)S(1)}, bf16[10,256,4096]{2,1,0:T(8,128)(2,1)}, f32[20,10,256,256]{3,2,1,0:T(8,128)}, f32[20,10,256,256]{3,2,1,...) custom-call(bf16[10,256,8192]{2,1,0:T(8,128)(2,1)} %bitcast.1), custom_call_target="tpu_custom_call" | custom-call | flops 112742891520 | bytes 419430400 | tf_op jit(solution)/shard_map/pallas_call | solution.py:432
  527.6 2.8 copy.3

commit v7 on v6

--- a/solution.py
+++ b/solution.py
@@ -407,6 +407,17 @@
             each(lambda i: mixed_recv(b, i), lambda i: y_copy(b, i, lambda copy: copy.wait_send()))
 
         loop(0, nb, finish_y)
+
+
+def store(src, out, sem):
+    parts = sem.shape[0]
+    size = src.shape[0] // parts
+    copies = [pltpu.make_async_copy(src.at[pl.ds(p * size, size)], out.at[pl.ds(p * size, size)], sem.at[p])
+              for p in range(parts)]
+    for copy in copies:
+        copy.start()
+    for copy in copies:
+        copy.wait()
 
 
 def solution(mesh):
@@ -454,7 +465,15 @@
             cost_estimate=pl.CostEstimate(flops=210 * 2 * BLOCK * BLOCK * half, bytes_accessed=400 * 2**20,
                                           transcendentals=0),
         )(a_local.reshape(nb, BLOCK, m_local))
-        return outs[0]
+        return pl.pallas_call(
+            store,
+            out_shape=shapes[0],
+            in_specs=[hbm],
+            out_specs=hbm,
+            scratch_shapes=[dma((4,))],
+            compiler_params=pltpu.CompilerParams(vmem_limit_bytes=2**20),
+            cost_estimate=pl.CostEstimate(flops=0, bytes_accessed=2 * shapes[0].size * 2, transcendentals=0),
+        )(outs[0])
 
     part_spec = P(("batch", "row"), "col")
     return jax.shard_map(local_fn, mesh=mesh, in_specs=(part_spec,), out_specs=part_spec, check_vma=False)

time: 534 us -> 534 us (level)
  no operation moved by 1% of the time
where the time goes in v7:
time: 534 us; the launch traced here: 530 us
  Pallas kernels  530 us (99%)
    pallas_call x1, Pallas kernels, local_fn(): pl.pallas_call(kernel, out_shape=shapes, in_specs=[hbm], out_specs=[hbm]...  528 us

profile of v7, /device:TPU:1, one launch (start us, length us, event | category | flops | bytes accessed | tf_op | source)
XLA Modules:
  0.0 530.4 jit_solution(3969049020377396199)
XLA Ops:
  0.0 527.6 %shard_map.17 = (bf16[2560,1280]{1,0:T(8,128)(2,1)S(1)}, bf16[10,256,4096]{2,1,0:T(8,128)(2,1)}, f32[20,10,256,256]{3,2,1,0:T(8,128)}, f32[20,10,256,256]{3,2,1,...) custom-call(bf16[10,256,8192]{2,1,0:T(8,128)(2,1)} %bitcast.1), custom_call_target="tpu_custom_call" | custom-call | flops 112742891520 | bytes 419430400 | tf_op jit(solution)/shard_map/pallas_call | solution.py:443
  527.6 2.8 shard_map.18

commit v8 on v6

--- a/solution.py
+++ b/solution.py
@@ -27,7 +27,7 @@
     lax.fori_loop(lower, upper, step, 0)
 
 
-def kernel(a, out, got_a, got_core, got_x, got_y, kept, ready, moved, relayed, own, part, other, cols, rows, extra, last_y,
+def kernel(a, out, got_a, got_core, got_x, got_y, kept, ready, moved, relayed, own, part, other, cols, extra, last_y,
            load_sem, far_sem, send_a, recv_a, send_core, recv_core, send_x, recv_x, send_y, recv_y, send_m, recv_m):
     nb = a.shape[0]
     cb = nb // 2
@@ -91,7 +91,12 @@
     first = fetch(a.at[:, :, pl.ds(pl.multiple_of(y * half, half), half)], own.at[pl.ds(0, nb)])
 
     def far_slot(lo, i):
-        return nb + 1 + jnp.where(i == lo, lax.rem(lo, 2), 2 + lax.rem(i, 2))
+        count = lo * (nb - 1) - lax.div(lo * (lo - 1), 2) + i - lo - 1
+        return nb + 1 + jnp.where(i == lo, lax.rem(lo, 2), 2 + lax.rem(jnp.maximum(count, 0), 3))
+
+    def far_next(lo, i):
+        last = i == nb - 1
+        return jnp.where(last, lo + 1, lo), jnp.where(last, lo + 1, i + 1)
 
     def far_copy(lo, i):
         slot = far_slot(lo, i)
@@ -99,6 +104,7 @@
                                      far_sem.at[slot - nb - 1])
 
     far_copy(jnp.int32(0), jnp.int32(0)).start()
+    far_copy(jnp.int32(0), jnp.int32(1)).start()
 
     def core_copy(job, h):
         slot = lax.rem(job, RING)
@@ -151,11 +157,11 @@
 
         def one(i):
             far_copy(lo, i).wait()
-            last = i == nb - 1
-
-            @pl.when(jnp.logical_or(jnp.logical_not(last), lo < nb - 1))
+            ahead = far_next(*far_next(lo, i))
+
+            @pl.when(ahead[0] < nb)
             def _():
-                far_copy(jnp.where(last, lo + 1, lo), jnp.where(last, lo + 1, i + 1)).start()
+                far_copy(*ahead).start()
 
             part[slot, i] = dot_t(own[i], own[lo]) + dot_t(own[far_slot(lo, i)], own[far_slot(lo, lo)])
 
@@ -378,16 +384,23 @@
             def _():
                 y_copy(hi, 2 * s + x, lambda copy: copy.wait_recv())
 
+        def store_block(hi, s):
+            span = pl.ds(s * BLOCK, BLOCK)
+            return fetch(cols.at[span], out.at[pl.ds(pl.multiple_of(hi * BLOCK, BLOCK), BLOCK), span], s)
+
         def final(hi):
             mine = fetch(kept.at[hi], other.at[pl.ds(0, cb)], 0)
             loop(0, cb, lambda s: wait_y(hi, s))
             theirs = fetch(got_y.at[hi], other.at[pl.ds(cb, cb)], 1)
             mine.wait()
             theirs.wait()
+            stores = []
             for s in range(cb):
-                rows[:, s * BLOCK:(s + 1) * BLOCK] = jnp.where(
-                    2 * s + x < hi + y, other[s] + other[cb + s], 0.0).astype(rows.dtype)
-            fetch(rows, out.at[pl.ds(pl.multiple_of(hi * BLOCK, BLOCK), BLOCK), :]).wait()
+                cols[s * BLOCK:(s + 1) * BLOCK, :] = jnp.where(
+                    2 * s + x < hi + y, other[s] + other[cb + s], 0.0).astype(cols.dtype)
+                stores.append(store_block(hi, s))
+            for store in stores:
+                store.wait()
 
         loop(0, nb - 1, final)
         mixed_reduce(jnp.int32(nb - 1))
@@ -395,9 +408,9 @@
         stores = []
         for s in range(cb):
             wait_y(nb - 1, s)
-            span = pl.ds(s * BLOCK, BLOCK)
-            rows[:, span] = jnp.where(2 * s + x < nb - 1 + y, part[0, s] + last_y[s], 0.0).astype(rows.dtype)
-            stores.append(fetch(rows.at[:, span], out.at[pl.ds((nb - 1) * BLOCK, BLOCK), span], s))
+            cols[s * BLOCK:(s + 1) * BLOCK, :] = jnp.where(
+                2 * s + x < nb - 1 + y, part[0, s] + last_y[s], 0.0).astype(cols.dtype)
+            stores.append(store_block(nb - 1, s))
         for store in stores:
             store.wait()
 
@@ -435,14 +448,13 @@
             in_specs=[hbm],
             out_specs=[hbm] * len(shapes),
             scratch_shapes=[
-                pltpu.VMEM((nb + 5, BLOCK, half), bf16),
+                pltpu.VMEM((nb + 6, BLOCK, half), bf16),
                 pltpu.VMEM((RING, nb, BLOCK, BLOCK), f32),
                 pltpu.VMEM((nb, BLOCK, BLOCK), f32),
                 pltpu.VMEM((local_rows, BLOCK), bf16),
-                pltpu.VMEM((BLOCK, cb * BLOCK), bf16),
                 pltpu.VMEM((2, nb, BLOCK, LANES), bf16),
                 pltpu.VMEM((cb, BLOCK, BLOCK), f32),
-                dma((cb,)), dma((4,)),
+                dma((cb,)), dma((5,)),
                 dma((nb,)), dma((nb,)),
                 dma((RING, 2)), dma((2 * nb, 2)),
                 dma((RING, nb)), dma((2 * nb, nb)),

time: 534 us -> 532 us (level)
  no operation moved by 1% of the time
where the time goes in v8:
time: 532 us; the launch traced here: 530 us
  Pallas kernels  528 us (99%)
    pallas_call x1, Pallas kernels, local_fn(): pl.pallas_call(kernel, out_shape=shapes, in_specs=[hbm], out_specs=[hbm]...  528 us

profile of v8, /device:TPU:1, one launch (start us, length us, event | category | flops | bytes accessed | tf_op | source)
XLA Modules:
  0.0 530.4 jit_solution(7270893766980001827)
XLA Ops:
  0.0 527.6 %shard_map.17 = (bf16[2560,1280]{1,0:T(8,128)(2,1)S(1)}, bf16[10,256,4096]{2,1,0:T(8,128)(2,1)}, f32[20,10,256,256]{3,2,1,0:T(8,128)}, f32[20,10,256,256]{3,2,1,...) custom-call(bf16[10,256,8192]{2,1,0:T(8,128)(2,1)} %bitcast.1), custom_call_target="tpu_custom_call" | custom-call | flops 112742891520 | bytes 419430400 | tf_op jit(solution)/shard_map/pallas_call | solution.py:445
  527.6 2.8 copy.3

commit v9 on v8

--- a/solution.py
+++ b/solution.py
@@ -27,7 +27,7 @@
     lax.fori_loop(lower, upper, step, 0)
 
 
-def kernel(a, out, got_a, got_core, got_x, got_y, kept, ready, moved, relayed, own, part, other, cols, extra, last_y,
+def kernel(a, out, got_a, got_core, got_x, got_y, kept, ready, moved, relayed, own, part, other, cols, extra,
            load_sem, far_sem, send_a, recv_a, send_core, recv_core, send_x, recv_x, send_y, recv_y, send_m, recv_m):
     nb = a.shape[0]
     cb = nb // 2
@@ -124,7 +124,7 @@
 
         @pl.when(b == nb - 1)
         def _():
-            action(remote(part.at[(2 * nb - 1) % RING, i], last_y.at[s], send_y.at[b, s], recv_y.at[b, s], y_dev))
+            action(remote(part.at[(2 * nb - 1) % RING, i], ready.at[nb - 1, cb + s], send_y.at[b, s], recv_y.at[b, s], y_dev))
 
     def add_other(slot, lower, upper):
         def one(i):
@@ -265,7 +265,9 @@
         @pl.when(jnp.logical_and(jnp.logical_not(same), lax.rem(b, 2) == x))
         def _():
             add_other(slot, split, nb)
+            last = fetch(part.at[slot, nb - 1], ready.at[nb - 1, lax.div(b, 2)], 1)
             fetch(part.at[slot], kept.at[:, lax.div(b, 2)]).wait()
+            last.wait()
 
         @pl.when(same)
         def _():
@@ -404,15 +406,7 @@
 
         loop(0, nb - 1, final)
         mixed_reduce(jnp.int32(nb - 1))
-        fetch(kept.at[nb - 1], part.at[0, pl.ds(0, cb)]).wait()
-        stores = []
-        for s in range(cb):
-            wait_y(nb - 1, s)
-            cols[s * BLOCK:(s + 1) * BLOCK, :] = jnp.where(
-                2 * s + x < nb - 1 + y, part[0, s] + last_y[s], 0.0).astype(cols.dtype)
-            stores.append(store_block(nb - 1, s))
-        for store in stores:
-            store.wait()
+        loop(0, cb, lambda s: wait_y(nb - 1, s))
 
     @pl.when(same)
     def _():
@@ -420,6 +414,56 @@
             each(lambda i: mixed_recv(b, i), lambda i: y_copy(b, i, lambda copy: copy.wait_send()))
 
         loop(0, nb, finish_y)
+
+
+def store(most, sums, out, mine, theirs, cols, read_sem, bulk_sem, write_sem):
+    nb = sums.shape[0]
+    cb = nb // 2
+    y = lax.axis_index("row")
+    c = lax.axis_index("col")
+    x = lax.div(c, 2)
+    same = lax.rem(c, 2) == y
+    head = (nb - 1) * BLOCK
+
+    def reads(s):
+        return [pltpu.make_async_copy(sums.at[nb - 1, s], mine.at[s], read_sem.at[0, s]),
+                pltpu.make_async_copy(sums.at[nb - 1, cb + s], theirs.at[s], read_sem.at[1, s])]
+
+    @pl.when(jnp.logical_not(same))
+    def _():
+        for s in range(cb):
+            for copy in reads(s):
+                copy.start()
+
+    parts = bulk_sem.shape[0] - 1
+    bulk = [pltpu.make_async_copy(most.at[pl.ds(p * head // parts, head // parts)],
+                                  out.at[pl.ds(p * head // parts, head // parts)], bulk_sem.at[p])
+            for p in range(parts)]
+    for copy in bulk:
+        copy.start()
+
+    @pl.when(same)
+    def _():
+        last = pltpu.make_async_copy(most.at[pl.ds(head, BLOCK)], out.at[pl.ds(head, BLOCK)], bulk_sem.at[parts])
+        last.start()
+        last.wait()
+
+    @pl.when(jnp.logical_not(same))
+    def _():
+        writes = []
+        for s in range(cb):
+            for copy in reads(s):
+                copy.wait()
+            cols[s] = jnp.where(2 * s + x < nb - 1 + y, mine[s] + theirs[s], 0.0).astype(cols.dtype)
+            write = pltpu.make_async_copy(cols.at[s], out.at[pl.ds(head, BLOCK), pl.ds(s * BLOCK, BLOCK)],
+                                          write_sem.at[s])
+            write.start()
+            writes.append(write)
+        for write in writes:
+            write.wait()
+
+    for copy in bulk:
+        copy.wait()
 
 
 def solution(mesh):
@@ -453,7 +497,6 @@
                 pltpu.VMEM((nb, BLOCK, BLOCK), f32),
                 pltpu.VMEM((local_rows, BLOCK), bf16),
                 pltpu.VMEM((2, nb, BLOCK, LANES), bf16),
-                pltpu.VMEM((cb, BLOCK, BLOCK), f32),
                 dma((cb,)), dma((5,)),
                 dma((nb,)), dma((nb,)),
                 dma((RING, 2)), dma((2 * nb, 2)),
@@ -462,11 +505,24 @@
                 dma((2,)), dma((2,)),
             ],
             compiler_params=pltpu.CompilerParams(collective_id=0, has_side_effects=True,
-                                                 vmem_limit_bytes=46 * 2**20),
+                                                 vmem_limit_bytes=45 * 2**20),
             cost_estimate=pl.CostEstimate(flops=210 * 2 * BLOCK * BLOCK * half, bytes_accessed=400 * 2**20,
                                           transcendentals=0),
         )(a_local.reshape(nb, BLOCK, m_local))
-        return outs[0]
+        return pl.pallas_call(
+            store,
+            out_shape=shapes[0],
+            in_specs=[hbm] * 2,
+            out_specs=hbm,
+            scratch_shapes=[
+                pltpu.VMEM((cb, BLOCK, BLOCK), f32),
+                pltpu.VMEM((cb, BLOCK, BLOCK), f32),
+                pltpu.VMEM((cb, BLOCK, BLOCK), bf16),
+                dma((2, cb)), dma((4,)), dma((cb,)),
+            ],
+            compiler_params=pltpu.CompilerParams(vmem_limit_bytes=45 * 2**20),
+            cost_estimate=pl.CostEstimate(flops=0, bytes_accessed=2 * shapes[0].size * 2, transcendentals=0),
+        )(outs[0], outs[6])
 
     part_spec = P(("batch", "row"), "col")
     return jax.shard_map(local_fn, mesh=mesh, in_specs=(part_spec,), out_specs=part_spec, check_vma=False)

time: 532 us -> 534 us (level)
  no operation moved by 1% of the time
where the time goes in v9:
time: 534 us; the launch traced here: 532 us
  Pallas kernels  532 us (100%)
    pallas_call x1, Pallas kernels, local_fn(): pl.pallas_call(kernel, out_shape=shapes, in_specs=[hbm], out_specs=[hbm]...  528 us

profile of v9, /device:TPU:1, one launch (start us, length us, event | category | flops | bytes accessed | tf_op | source)
XLA Modules:
  0.0 532.0 jit_solution(1940428150319621292)
XLA Ops:
  0.0 527.5 %shard_map.17 = (bf16[2560,1280]{1,0:T(8,128)(2,1)S(1)}, bf16[10,256,4096]{2,1,0:T(8,128)(2,1)}, f32[20,10,256,256]{3,2,1,0:T(8,128)}, f32[20,10,256,256]{3,2,1,...) custom-call(bf16[10,256,8192]{2,1,0:T(8,128)(2,1)} %bitcast.1), custom_call_target="tpu_custom_call" | custom-call | flops 112742891520 | bytes 419430400 | tf_op jit(solution)/shard_map/pallas_call | solution.py:489
  527.5 4.4 shard_map.18
